TPU v7x, 256 devices: a whole 4x4x8 slice. The times are simulated.
256 devices in a mesh: dp: 16 (over y_hi, z), tensor: 16 (over y_lo, x, core).
Axes of the slice: x: 4, y: 4 (y_hi: 2, y_lo: 2; y = y_hi * 2 + y_lo), z: 8, core: 2. Of those that a mesh axis runs over, the one named last changes fastest.
Arguments:
- q_nope: bfloat16 [64, 2, 128, 128], P('dp', None, 'tensor'), parts along dimension 0, may hold values from -6 to 6
- q_rope: bfloat16 [64, 2, 128, 64], P('dp', None, 'tensor'), parts along dimension 0, may hold values from -8 to 8
- w_uk: bfloat16 [128, 128, 512], P('tensor'), may hold values from -0.5 to 0.5
- w_uv: bfloat16 [128, 512, 128], P('tensor'), may hold values from -0.25 to 0.25
- cache_latent: bfloat16 [64, 32768, 512], P('dp', 'tensor'), parts along dimension 0, may hold values from -4 to 4
- cache_rope: bfloat16 [64, 64, 32768], P('dp', None, 'tensor'), parts along dimension 0, may hold values from -14 to 14
- scale_pool: float32 [5, 16384], P(None, ('dp', 'tensor')), parts along dimension 1, may hold values from 0.3 to 3
- block_index: int32 [64, 256], P('dp', 'tensor'), parts along dimension 0, may hold values from 0 to 1023, as said below
- lengths: int32 [64], P('dp'), parts along dimension 0, may hold values from 8192 to 32768, as said below
Outputs:
- head_outputs: bfloat16 [64, 2, 128, 128], P('dp', None, 'tensor'), parts along dimension 0
There are 16 independent parts, one for each index of `dp`. A program takes and returns all parts, laid end to end along the dimension named above; an argument that names none is the same for every part. Nothing has to cross between parts.
Inputs may be any that keep to these rules, and one draw needn't show every extreme that they name: `block_index`: every column of the scale table is named by exactly one cache block of the group. `lengths`: in a group of two or more requests, one request is shorter than 16384 and the others are at least 16384 long.
All inputs are finite; a program needn't handle non-finite values.
Results may differ from a plain program's by a relative error of at most 0.012.
Values may be sent and summed in bfloat16 or wider, within the bound.
A program may use at most 128 MiB of HBM per device.

v0:
```python
import jax
import jax.numpy as jnp
from jax import lax
from jax.sharding import PartitionSpec as P

masked_score = -1e30


def copy_for_each(value, axis):
    copies = jnp.broadcast_to(value, (lax.axis_size(axis), *value.shape))
    return lax.all_to_all(copies, axis, split_axis=0, concat_axis=0, tiled=True)


def joined_along(tiles, dim):
    dims = list(tiles.shape[1:])
    dims[dim] *= tiles.shape[0]
    return jnp.moveaxis(tiles, 0, dim).reshape(dims)


def gather_directly(value, axis, dim):
    tiles = copy_for_each(value, axis)
    return joined_along(tiles, dim)


def sent_together(arrays, axis, dim, along):
    widths = [a.shape[along] for a in arrays]
    both = jnp.concatenate(arrays, axis=along)
    filled = gather_directly(both, axis, dim)
    return tuple(jnp.split(filled, [sum(widths[:k]) for k in range(1, len(widths))], axis=along))


def of_everyone(value, axis):
    everything = copy_for_each(value, axis)
    return jnp.max(everything, axis=0)


def local(q_nope, q_rope, w_uk, w_uv, cache_latent, cache_rope, scale_pool, block_index, lengths):
    requests, new_tokens, local_heads, nope_width = q_nope.shape
    rope_width = q_rope.shape[3]
    latent_width = w_uk.shape[2]
    local_span = cache_latent.shape[1]
    blocks = block_index.shape[1]
    block_width = local_span // blocks
    groups = scale_pool.shape[0]
    query_latent = jnp.einsum(
        "rthn,hnc->rthc", q_nope, w_uk, preferred_element_type=jnp.float32
    ).astype(jnp.bfloat16)
    every_latent, every_rope = sent_together((query_latent, q_rope), "tensor", 2, 3)
    scale_table = gather_directly(scale_pool, "tensor", 1)
    picked = jnp.take(scale_table, block_index, axis=1)
    latent_scale = jnp.transpose(picked[: groups - 1], (1, 2, 0))[:, :, None, :, None]
    latent_full = (
        (
            cache_latent.reshape(requests, blocks, block_width, groups - 1, -1).astype(jnp.float32)
            * latent_scale
        )
        .astype(jnp.bfloat16)
        .reshape(cache_latent.shape)
    )
    rope_scale = picked[groups - 1][:, None, :, None]
    rope_full = (
        (
            cache_rope.reshape(requests, rope_width, blocks, block_width).astype(jnp.float32)
            * rope_scale
        )
        .astype(jnp.bfloat16)
        .reshape(cache_rope.shape)
    )
    head_count = every_latent.shape[2]
    row_count = new_tokens * head_count
    latent_rows = every_latent.reshape(requests, row_count, latent_width)
    rope_rows = every_rope.reshape(requests, row_count, rope_width)
    scores = jnp.einsum(
        "rmc,rpc->rmp", latent_rows, latent_full, preferred_element_type=jnp.float32
    ) + jnp.einsum("rmd,rdp->rmp", rope_rows, rope_full, preferred_element_type=jnp.float32)
    scores = scores * (nope_width + rope_width) ** (-0.5)
    positions = lax.axis_index("tensor") * local_span + jnp.arange(local_span, dtype=jnp.int32)
    limits = lengths[:, None] - new_tokens + jnp.arange(new_tokens, dtype=jnp.int32)[None, :]
    allowed = positions[None, None, :] <= limits[:, :, None]
    allowed = jnp.repeat(allowed, head_count, axis=1)
    scores = jnp.where(allowed, scores, masked_score)
    peak_score = of_everyone(jnp.max(scores, axis=2), "tensor")
    weights = jnp.exp(scores - peak_score[:, :, None])
    totals = jnp.sum(weights, axis=2).reshape(requests, new_tokens, head_count)
    mixture = jnp.einsum(
        "rmp,rpc->rmc",
        weights.astype(jnp.bfloat16),
        latent_full,
        preferred_element_type=jnp.float32,
    )
    mixture = mixture.reshape(requests, new_tokens, head_count, latent_width)
    summed = jnp.sum(
        lax.all_to_all(mixture[None], "tensor", split_axis=3, concat_axis=0, tiled=True), axis=0
    )
    counted = jnp.sum(
        lax.all_to_all(totals[None, ..., None], "tensor", split_axis=3, concat_axis=0, tiled=True),
        axis=0,
    )
    attended = (summed / counted).astype(jnp.bfloat16)
    projected = jnp.einsum("rthc,hcv->rthv", attended, w_uv, preferred_element_type=jnp.float32)
    return projected.astype(jnp.bfloat16)


def solution(mesh):
    placed = (
        P("dp", None, "tensor", None),
        P("dp", None, "tensor", None),
        P("tensor", None, None),
        P("tensor", None, None),
        P("dp", "tensor", None),
        P("dp", None, "tensor"),
        P(None, ("dp", "tensor")),
        P("dp", "tensor"),
        P("dp"),
    )
    return jax.shard_map(
        local, mesh=mesh, in_specs=placed, out_specs=P("dp", None, "tensor", None), check_vma=False
    )
```

profile of v0, /device:TPU:1, one launch (start us, length us, event | category | flops | bytes accessed | tf_op | source)
XLA Modules:
  0.0 145.5 jit_solution(6926858440620674722)
XLA Ops:
  0.0 0.8 broadcast_in_dim.37
  1.5 6.8 %all-to-all-start.1 = ((f32[16,1,320]{2,1,0:T(1,128)}), f32[16,1,320]{2,1,0:T(1,128)S(1)}, u32[]{:S(2)}, u32[]{:S(2)}) async-start(f32[16,1,320]{2,1,0:T(1,128)} %reshape.76), calls=%async_computation.1 | async-start | bytes 49152 | tf_op jit(solution)/shard_map/all_to_all | solution.py:11
  9.1 0.7 copy.81
  10.5 1.0 fusion.5
  11.7 2.4 %all-to-all-done.1 = f32[16,1,320]{2,1,0:T(1,128)S(1)} async-done(((f32[16,1,320]{2,1,0:T(1,128)}), f32[16,1,320]{2,1,0:T(1,128)S(1)}, u32[]{:S(2)}, u32[]{:S(2)}) %all-to-all-start.1) | async-done | bytes 20512 | tf_op jit(solution)/shard_map/all_to_all | solution.py:11
  14.1 1.2 broadcast_in_dim.35
  15.3 3.9 %all-to-all-start = ((bf16[16,4,2,8,576]{4,3,2,1,0:T(8,128)(2,1)}), bf16[16,4,2,8,576]{4,3,2,1,0:T(8,128)(2,1)S(1)}, u32[]{:S(2)}, u32[]{:S(2)}) async-start(bf16[16,4,2,8,576]{4,3,2,1,0:T(8,128)(2,1)} %broadcast_in_dim.35), calls=%async_computation | async-start | bytes 2621440 | tf_op jit(solution)/shard_map/all_to_all | solution.py:11
  19.2 0.7 compare_and_fusion
  20.4 0.7 reduce.7
  22.2 6.1 %mul.36 = f32[4,16,128,4,128]{4,3,2,1,0:T(4,128)} broadcast(f32[4,16,4]{2,1,0:T(8,128)S(1)} %copy.86), dimensions={0,1,3} | broadcast | bytes 16778240 | tf_op jit(solution)/shard_map/mul | solution.py:54
  28.3 19.9 %mul.37 = f32[4,2048,512]{2,1,0:T(8,128)} reshape(f32[4,16,128,4,128]{4,3,2,1,0:T(4,128)} %mul.36) | data formatting | bytes 33554432 | tf_op jit(solution)/shard_map/mul | solution.py:54
  48.6 1.1 copy-done.2
  49.6 13.9 %fusion.13 = f32[4,256,2048]{2,1,0:T(8,128)} fusion(bf16[4,256,512]{2,1,0:T(8,128)(2,1)S(1)} %bitcast.46, f32[4,2048,512]{2,1,0:T(8,128)} %mul.37, bf16[4,2048,512]{2,1,0:T(8,128)(2,1)} %param.13), kind=kOutput, calls=%fused_computation.34 | convolution fusion | flops 2160066560 | bytes 34603008 | tf_op jit(solution)/shard_map/rmc,rpc->rmp/dot_general | solution.py:73
  63.5 8.6 %fusion.14 = (f32[4,256]{1,0:T(4,128)S(1)}, f32[4,256,2048]{2,1,0:T(8,128)}) fusion(f32[4,256,2048]{2,1,0:T(8,128)} %fusion.13, bf16[4,256,64]{2,1,0:T(8,128)(2,1)S(1)} %bitcast.45, bf16[4,64,2048]{2,1,0:T(8,128)(2,1)S(1)} %copy-done.3, f32[4,2048]{1,0:T(4,128)S(1)} %bitcast.50, pred[4,2,2048]{2,1,0:T(4,128)(4,1)S(1)} %broadcast_compare_fusion), kind=kOutput, calls=%fused_computation.35 | convolution fusion | flops 278395904 | bytes 18010112 | tf_op jit(solution)/shard_map/rmd,rdp->rmp/dot_general | solution.py:75
  72.1 11.4 %all_to_all.39 = f32[16,4,256]{2,1,0:T(4,128)S(1)} all-to-all(f32[16,4,256]{2,1,0:T(4,128)S(1)} %broadcast_in_dim.41), channel_id=1, replica_groups=mesh['dp'=16,'tensor'=16] {'tensor'}, dimensions={0} | all-to-all | bytes 131072 | tf_op jit(solution)/shard_map/all_to_all | solution.py:11
  83.5 4.6 %fusion = f32[4,256]{1,0:T(4,128)S(1)} fusion(f32[4,256,2048]{2,1,0:T(8,128)} %get-tuple-element.6, f32[4,256]{1,0:T(4,128)S(1)} %reduce_max.19), kind=kLoop, calls=%fused_computation.4 | loop fusion | flops 4193280 | bytes 8396800 | tf_op jit(solution)/shard_map/reduce_sum | solution.py:84
  88.2 0.8 copy.91
  89.0 3.7 %all-to-all-start.4 = ((f32[1,4,2,128,1]{1,2,4,0,3:T(2,128)}), f32[1,4,2,128,1]{1,2,4,0,3:T(2,128)S(1)}, u32[]{:S(2)}, u32[]{:S(2)}) async-start(f32[1,4,2,128,1]{1,2,4,0,3:T(2,128)} %copy.91), calls=%async_computation.4 | async-start | bytes 262144 | tf_op jit(solution)/shard_map/all_to_all | solution.py:96
  92.7 13.1 %fusion.2 = f32[4,256,512]{2,1,0:T(8,128)S(1)} fusion(f32[4,256,2048]{2,1,0:T(8,128)} %get-tuple-element.6, f32[4,256]{1,0:T(4,128)S(1)} %reduce_max.19, f32[4,2048,512]{2,1,0:T(8,128)} %mul.37, bf16[4,2048,512]{2,1,0:T(8,128)(2,1)} %param.13), kind=kOutput, calls=%fused_computation.6 | convolution fusion | flops 2164260864 | bytes 35655680 | tf_op jit(solution)/shard_map/rmp,rpc->rmc/dot_general | solution.py:85
  105.8 3.0 %copy.89 = f32[1,4,2,128,512]{4,2,1,0,3:T(2,128)} copy(f32[1,4,2,128,512]{4,3,2,1,0:T(8,128)S(1)} %bitcast.43) | data formatting | bytes 4194304 | tf_op jit(solution)/shard_map/broadcast_in_dim;reshape | solution.py:93
  108.8 5.8 %all-to-all-start.3 = ((f32[1,4,2,128,512]{4,2,1,0,3:T(2,128)}), f32[1,4,2,128,512]{4,2,1,0,3:T(2,128)S(1)}, u32[]{:S(2)}, u32[]{:S(2)}) async-start(f32[1,4,2,128,512]{4,2,1,0,3:T(2,128)} %copy.89), calls=%async_computation.3 | async-start | bytes 4194304 | tf_op jit(solution)/shard_map/all_to_all | solution.py:93
  114.8 27.4 %all-to-all-done.3 = f32[1,4,2,128,512]{4,2,1,0,3:T(2,128)S(1)} async-done(((f32[1,4,2,128,512]{4,2,1,0,3:T(2,128)}), f32[1,4,2,128,512]{4,2,1,0,3:T(2,128)S(1)}, u32[]{:S(2)}, u32[]{:S(2)}) %all-to-all-start.3) | async-done | bytes 2097184 | tf_op jit(solution)/shard_map/all_to_all | solution.py:93
  142.2 1.1 reduce_sum.27
  143.4 1.5 %fusion.6 = bf16[4,2,8,128]{3,0,1,2:T(4,128)(2,1)S(1)} fusion(bf16[8,512,128]{2,1,0:T(8,128)(2,1)} %param.12, bf16[4,2,8,512]{3,2,1,0:T(8,128)(2,1)S(1)} %fusion.10), kind=kOutput, calls=%fused_computation.13 | convolution fusion | flops 8396800 | bytes 1130496 | tf_op jit(solution)/shard_map/rthc,hcv->rthv/dot_general | solution.py:100
  (40 shorter events, 5.2 us)
Async XLA Ops:
  0.0 10.5 %copy-start = (bf16[8,128,512]{2,1,0:T(8,128)(2,1)S(1)}, bf16[8,128,512]{2,1,0:T(8,128)(2,1)}, u32[]{:S(2)}) copy-start(bf16[8,128,512]{2,1,0:T(8,128)(2,1)} %param.11) | copy-start | bytes 3145732
  1.5 12.6 %all-to-all-start.1 = ((f32[16,1,320]{2,1,0:T(1,128)}), f32[16,1,320]{2,1,0:T(1,128)S(1)}, u32[]{:S(2)}, u32[]{:S(2)}) async-start(f32[16,1,320]{2,1,0:T(1,128)} %reshape.76), calls=%async_computation.1 | async-start | bytes 49152 | tf_op jit(solution)/shard_map/all_to_all | solution.py:11
  15.3 33.0 %all-to-all-start = ((bf16[16,4,2,8,576]{4,3,2,1,0:T(8,128)(2,1)}), bf16[16,4,2,8,576]{4,3,2,1,0:T(8,128)(2,1)S(1)}, u32[]{:S(2)}, u32[]{:S(2)}) async-start(bf16[16,4,2,8,576]{4,3,2,1,0:T(8,128)(2,1)} %broadcast_in_dim.35), calls=%async_computation | async-start | bytes 2621440 | tf_op jit(solution)/shard_map/all_to_all | solution.py:11
  48.5 1.2 copy-start.2
  49.6 13.9 %slice-start = ((bf16[4,2,128,576]{3,2,1,0:T(8,128)(2,1)}), bf16[4,2,128,64]{3,2,1,0:T(8,128)(2,1)S(1)}, s32[]{:S(2)}) async-start(bf16[4,2,128,576]{3,2,1,0:T(8,128)(2,1)} %copy-done.2), calls=%async_computation.5 | async-start | bytes 524288 | tf_op jit(solution)/shard_map/split | solution.py:29
  49.6 13.9 %copy-start.3 = (bf16[4,64,2048]{2,1,0:T(8,128)(2,1)S(1)}, bf16[4,64,2048]{2,1,0:T(8,128)(2,1)}, u32[]{:S(2)}) copy-start(bf16[4,64,2048]{2,1,0:T(8,128)(2,1)} %param.14) | copy-start | bytes 3145732
  89.0 19.8 %all-to-all-start.4 = ((f32[1,4,2,128,1]{1,2,4,0,3:T(2,128)}), f32[1,4,2,128,1]{1,2,4,0,3:T(2,128)S(1)}, u32[]{:S(2)}, u32[]{:S(2)}) async-start(f32[1,4,2,128,1]{1,2,4,0,3:T(2,128)} %copy.91), calls=%async_computation.4 | async-start | bytes 262144 | tf_op jit(solution)/shard_map/all_to_all | solution.py:96
  92.7 52.8 %copy-start.1 = (bf16[8,128,512]{2,1,0:T(8,128)(2,1)S(1)}, bf16[8,128,512]{2,1,0:T(8,128)(2,1)}, u32[]{:S(2)}) copy-start(bf16[8,128,512]{2,1,0:T(8,128)(2,1)} %param.11) | copy-start | bytes 3145732
  108.8 33.4 %all-to-all-start.3 = ((f32[1,4,2,128,512]{4,2,1,0,3:T(2,128)}), f32[1,4,2,128,512]{4,2,1,0,3:T(2,128)S(1)}, u32[]{:S(2)}, u32[]{:S(2)}) async-start(f32[1,4,2,128,512]{4,2,1,0,3:T(2,128)} %copy.89), calls=%async_computation.3 | async-start | bytes 4194304 | tf_op jit(solution)/shard_map/all_to_all | solution.py:93
where the time goes:
time: 147 us; the launch traced here: 146 us
  matrix products  38 us (26%)
  local copies, waits for them, and re-layouts  37 us (25%)
  waiting for transfers between devices  29.8 us (20%)
  starting transfers between devices  20.2 us (14%)
  blocking collectives  11.4 us (8%)
  other arithmetic  8.91 us (6%)
    all_to_all x1, waiting for transfers between devices, local(): lax.all_to_all(mixture[None], 'tensor', split_axis=3, concat_axis=0, tile...  27.4 us
    mul x2, local copies, waits for them, and re-layouts, local(): cache_latent.reshape(requests, blocks, block_width, groups - 1, -1)  26 us
    dot_general x1, matrix products, local(): jnp.einsum('rmc,rpc->rmp', latent_rows, latent_full, preferred_element_ty...  13.9 us
    dot_general x1, matrix products, local(): jnp.einsum('rmp,rpc->rmc', weights.astype(jnp.bfloat16), latent_full, pre...  13.1 us
    all_to_all x1, blocking collectives, copy_for_each(): return lax.all_to_all(copies, axis, split_axis=0, concat_axis=0, tiled=True)  11.4 us
    all_to_all x2, starting transfers between devices, copy_for_each(): return lax.all_to_all(copies, axis, split_axis=0, concat_axis=0, tiled=True)  10.7 us
    dot_general x1, matrix products, local(): jnp.einsum('rmd,rdp->rmp', rope_rows, rope_full, preferred_element_type=j...  8.58 us
    all_to_all x1, starting transfers between devices, local(): lax.all_to_all(mixture[None], 'tensor', split_axis=3, concat_axis=0, tile...  5.8 us
  transfers between devices with their start and end apart: 4, of which 2 were waited for; matrix products, arithmetic and copies ran while one was open for 33% of the time, Pallas kernels for 0%

commit v1 on v0

v1 whole, which is shorter than its diff:
```python
import functools
import math

import jax
import jax.numpy as jnp
from jax import lax
from jax.experimental import pallas as pl
from jax.experimental.pallas import tpu as pltpu
from jax.sharding import PartitionSpec as P

MESH = pl.DeviceIdType.MESH
R, T, H = 4, 2, 8
ROWS, LAT, ROPE, WIDE = 256, 512, 64, 640
SPAN, BLOCKS = 2048, 16
X, CHIPS = 4, 8
FACTOR = (128 + 64) ** -0.5 * math.log2(math.e)
MASKED = -1e30
F32, BF16 = jnp.float32, jnp.bfloat16


def parts_of(value, count):
    parts = []
    for _ in range(count):
        part = value.astype(BF16).astype(F32)
        parts.append(part)
        value = value - part
    return parts


def stats_tile(peak, total):
    lane = lax.broadcasted_iota(jnp.int32, (peak.shape[0], 128), 1)
    tile = jnp.zeros((peak.shape[0], 128), F32)
    for at, part in enumerate(parts_of(peak, 3) + parts_of(total, 2)):
        tile = jnp.where(lane == at, part, tile)
    return tile.astype(BF16)


def stats_of(tile):
    tile = tile.astype(F32)
    return tile[:, 0:1] + tile[:, 1:2] + tile[:, 2:3], tile[:, 3:4] + tile[:, 4:5]


def kernel(
    q_nope, q_rope, w_uk, w_uv, latent, rope, pool, index, lengths, out,
    nope_v, qrope_v, uk_v, uv_v, lat, rop, table, table_s, index_s, length_s,
    qf, flat, queries, scores, weights, mixed, peaks, sums, out_a, in_a, out_b, in_b, att, res, res_b,
    load_sem, table_sem, table_send, table_recv, q_send, q_recv, f_send, f_recv,
    a_send, a_recv, b_send, b_recv, out_sem,
):
    me = lax.axis_index("tensor")
    core = lax.rem(me, 2)
    chip = me // 2
    row, column = chip // X, lax.rem(chip, X)
    partner = me + 1 - 2 * core

    def peer(j, sign):
        dy, dx = j // X, j % X
        other = lax.rem(row + dy, 2) * X + lax.rem(column + (dx if sign > 0 else X - dx), X)
        return other * 2 + core

    def remote(src, dst, send, recv, to):
        return pltpu.make_async_remote_copy(
            src_ref=src, dst_ref=dst, send_sem=send, recv_sem=recv,
            device_id={"tensor": to}, device_id_type=MESH,
        )

    barrier = pltpu.get_barrier_semaphore()
    for step in range(1, 16):
        pl.semaphore_signal(
            barrier, inc=1, device_id={"tensor": lax.rem(me + step, 16)}, device_id_type=MESH
        )

    small = [
        pltpu.make_async_copy(w_uk, uk_v, load_sem.at[0]),
        pltpu.make_async_copy(q_nope, nope_v, load_sem.at[1]),
        pltpu.make_async_copy(q_rope, qrope_v, load_sem.at[2]),
        pltpu.make_async_copy(pool, table.at[0], load_sem.at[3]),
        pltpu.make_async_copy(index, index_s, load_sem.at[4]),
        pltpu.make_async_copy(lengths, length_s, load_sem.at[5]),
    ]
    big = []
    for r in range(R):
        big.append(pltpu.make_async_copy(latent.at[r], lat.at[r], load_sem.at[6 + r]))
        big.append(pltpu.make_async_copy(rope.at[r], rop.at[r], load_sem.at[10 + r]))
    late = pltpu.make_async_copy(w_uv, uv_v, load_sem.at[14])
    for copy in small + big + [late]:
        copy.start()
    for copy in small:
        copy.wait()

    qf[...] = nope_v[...].astype(F32).reshape(R * T * H, 128)
    for h in range(H):
        rows = qf[pl.ds(h, R * T, stride=H), :].astype(BF16)
        got = jnp.dot(rows, uk_v[h], preferred_element_type=F32)
        for g in range(4):
            flat[g, pl.ds(h, R * T, stride=H), :] = got[:, 128 * g : 128 * (g + 1)]
    for r in range(R):
        for g in range(4):
            queries[r, 0:16, 128 * g : 128 * (g + 1)] = flat[g, 16 * r : 16 * (r + 1), :].astype(BF16)
        turned = qrope_v[r].astype(F32).reshape(16, ROPE)
        queries[r, 0:16, LAT:WIDE] = jnp.concatenate([turned, jnp.zeros((16, 64), F32)], axis=1).astype(BF16)

    pl.semaphore_wait(barrier, 15)

    table_copies = []
    for step in range(1, 16):
        table_copies.append(
            remote(table.at[0], table.at[step], table_send.at[step - 1], table_recv.at[step - 1],
                   lax.rem(me + 16 - step, 16))
        )
    for copy in table_copies:
        copy.start()
    q_copies = []
    for r in range(R):
        q_copies.append([
            remote(queries.at[r, pl.ds(0, 16)], queries.at[r, pl.ds(16 * j, 16)],
                   q_send.at[r, j - 1], q_recv.at[r, j - 1], peer(j, -1))
            for j in range(1, CHIPS)
        ])
        for copy in q_copies[r]:
            copy.start()
    f_copies = [
        remote(queries.at[r, pl.ds(0, 128)], queries.at[r, pl.ds(128, 128)],
               f_send.at[r], f_recv.at[r], partner)
        for r in range(R)
    ]
    a_copies = [
        remote(out_a.at[r], in_a.at[r], a_send.at[r], a_recv.at[r], partner) for r in range(R)
    ]
    b_copies = [
        [
            remote(out_b.at[r, pl.ds(16 * j, 16)], in_b.at[r, pl.ds(16 * j, 16)],
                   b_send.at[r, j - 1], b_recv.at[r, j - 1], peer(j, 1))
            for j in range(1, CHIPS)
        ]
        for r in range(R)
    ]

    for copy in table_copies:
        copy.wait_recv()
    to_scalar = pltpu.make_async_copy(table, table_s, table_sem)
    to_scalar.start()
    to_scalar.wait()

    def scale(r):
        big[2 * r].wait()
        big[2 * r + 1].wait()

        def one(b, carry):
            at = index_s[r, b]
            slot = lax.rem(at // 64 + 16 - me, 16)
            col = lax.rem(at, 64)
            rows = pl.ds(pl.multiple_of(b * 128, 128), 128)
            for g in range(4):
                lat[r, rows, 128 * g : 128 * (g + 1)] = (
                    lat[r, rows, 128 * g : 128 * (g + 1)].astype(F32) * table_s[slot, g, col]
                ).astype(BF16)
            rop[r, :, rows] = (rop[r, :, rows].astype(F32) * table_s[slot, 4, col]).astype(BF16)
            return carry

        lax.fori_loop(0, BLOCKS, one, 0)

    WIDTH = 512
    CHUNKS = SPAN // WIDTH

    def attend(r):
        length = length_s[r]

        def score(n, top):
            cols = pl.ds(pl.multiple_of(n * WIDTH, WIDTH), WIDTH)
            got = lax.dot_general(
                queries[r, :, 0:LAT], lat[r, cols, :], (((1,), (1,)), ((), ())),
                preferred_element_type=F32,
            ) + jnp.dot(queries[r, :, LAT : LAT + ROPE], rop[r, :, cols], preferred_element_type=F32)
            place = lax.broadcasted_iota(jnp.int32, (1, T, 8, WIDTH), 3) + (me * SPAN + n * WIDTH)
            limit = length - T + lax.broadcasted_iota(jnp.int32, (1, T, 8, WIDTH), 1)
            got = jnp.where(place <= limit, got.reshape(16, T, 8, WIDTH), MASKED).reshape(ROWS, WIDTH)
            scores[:, cols] = got
            for g in range(WIDTH // 128):
                top = jnp.maximum(top, got[:, 128 * g : 128 * (g + 1)])
            return top

        top = lax.fori_loop(0, CHUNKS, score, jnp.full((ROWS, 128), -3e38, F32))
        peak = jnp.max(top, axis=1, keepdims=True)

        def weigh(n, total):
            cols = pl.ds(pl.multiple_of(n * WIDTH, WIDTH), WIDTH)
            got = jnp.exp2((scores[:, cols] - peak) * FACTOR)
            weights[:, cols] = got.astype(BF16)
            for g in range(WIDTH // 128):
                total = total + got[:, 128 * g : 128 * (g + 1)]
            return total

        total = lax.fori_loop(0, CHUNKS, weigh, jnp.zeros((ROWS, 128), F32))
        total = jnp.sum(total, axis=1, keepdims=True)
        got = jnp.dot(weights[...], lat[r], preferred_element_type=F32)
        out_a[r, :, 0:LAT] = got[128:].astype(BF16)
        out_a[r, :, LAT:WIDE] = stats_tile(peak[128:], total[128:])
        a_copies[r].start()
        mixed[r] = got[:128]
        peaks[r] = jnp.broadcast_to(peak[:128], (128, 128))
        sums[r] = jnp.broadcast_to(total[:128], (128, 128))

    def combine(r):
        a_copies[r].wait_recv()
        peak_0, total_0 = peaks[r, :, 0:1], sums[r, :, 0:1]
        peak_1, total_1 = stats_of(in_a[r, :, LAT:WIDE])
        peak = jnp.maximum(peak_0, peak_1)
        gain_0 = jnp.exp2((peak_0 - peak) * FACTOR)
        gain_1 = jnp.exp2((peak_1 - peak) * FACTOR)
        out_b[r, :, 0:LAT] = (mixed[r] * gain_0 + in_a[r, :, 0:LAT].astype(F32) * gain_1).astype(BF16)
        out_b[r, :, LAT:WIDE] = stats_tile(peak, total_0 * gain_0 + total_1 * gain_1)
        for copy in b_copies[r]:
            copy.start()

    def finish(r):
        for copy in b_copies[r]:
            copy.wait_recv()
        found = [stats_of(out_b[r, 0:16, LAT:WIDE])] + [
            stats_of(in_b[r, 16 * j : 16 * (j + 1), LAT:WIDE]) for j in range(1, CHIPS)
        ]
        peak = functools.reduce(jnp.maximum, [p for p, _ in found])
        total = jnp.zeros((16, 1), F32)
        summed = jnp.zeros((16, LAT), F32)
        for j, (p, t) in enumerate(found):
            gain = jnp.exp2((p - peak) * FACTOR)
            total = total + t * gain
            block = out_b[r, 0:16, 0:LAT] if j == 0 else in_b[r, 16 * j : 16 * (j + 1), 0:LAT]
            summed = summed + block.astype(F32) * gain
        attended = summed / total
        for g in range(4):
            att[g, 16 * r : 16 * (r + 1), :] = attended[:, 128 * g : 128 * (g + 1)]

    for r in range(R):
        for copy in q_copies[r]:
            copy.wait_recv()
        f_copies[r].start()
        scale(r)
        f_copies[r].wait_recv()
        attend(r)
        if r >= 1:
            combine(r - 1)
    combine(R - 1)
    for r in range(R):
        finish(r)

    late.wait()
    for h in range(H):
        rows = jnp.concatenate(
            [att[g, pl.ds(h, R * T, stride=H), :] for g in range(4)], axis=1
        ).astype(BF16)
        res[pl.ds(h, R * T, stride=H), :] = jnp.dot(rows, uv_v[h], preferred_element_type=F32)
    res_b[...] = res[...].reshape(R, T, H, 128).astype(BF16)
    done = pltpu.make_async_copy(res_b, out, out_sem)
    done.start()

    for copy in table_copies:
        copy.wait_send()
    for r in range(R):
        for copy in q_copies[r] + b_copies[r] + [f_copies[r], a_copies[r]]:
            copy.wait_send()
    done.wait()


def local(*args):
    dma = pltpu.SemaphoreType.DMA
    return pl.pallas_call(
        kernel,
        out_shape=jax.ShapeDtypeStruct((R, T, H, 128), BF16),
        in_specs=[pl.BlockSpec(memory_space=pl.ANY)] * 9,
        out_specs=pl.BlockSpec(memory_space=pl.ANY),
        scratch_shapes=[
            pltpu.VMEM((R, T, H, 128), BF16),
            pltpu.VMEM((R, T, H, ROPE), BF16),
            pltpu.VMEM((H, 128, LAT), BF16),
            pltpu.VMEM((H, LAT, 128), BF16),
            pltpu.VMEM((R, SPAN, LAT), BF16),
            pltpu.VMEM((R, ROPE, SPAN), BF16),
            pltpu.VMEM((16, 5, 64), F32),
            pltpu.SMEM((16, 5, 64), F32),
            pltpu.SMEM((R, BLOCKS), jnp.int32),
            pltpu.SMEM((R,), jnp.int32),
            pltpu.VMEM((R * T * H, 128), F32),
            pltpu.VMEM((4, R * T * H, 128), F32),
            pltpu.VMEM((R, ROWS, WIDE), BF16),
            pltpu.VMEM((ROWS, SPAN), F32),
            pltpu.VMEM((ROWS, SPAN), BF16),
            pltpu.VMEM((R, 128, LAT), F32),
            pltpu.VMEM((R, 128, 128), F32),
            pltpu.VMEM((R, 128, 128), F32),
            pltpu.VMEM((R, 128, WIDE), BF16),
            pltpu.VMEM((R, 128, WIDE), BF16),
            pltpu.VMEM((R, 128, WIDE), BF16),
            pltpu.VMEM((R, 128, WIDE), BF16),
            pltpu.VMEM((4, R * T * H, 128), F32),
            pltpu.VMEM((R * T * H, 128), F32),
            pltpu.VMEM((R, T, H, 128), BF16),
            dma((15,)),
            dma(()),
            dma((15,)),
            dma((15,)),
            dma((R, 7)),
            dma((R, 7)),
            dma((R,)),
            dma((R,)),
            dma((R,)),
            dma((R,)),
            dma((R, 7)),
            dma((R, 7)),
            dma(()),
        ],
        compiler_params=pltpu.CompilerParams(collective_id=0, has_side_effects=True),
        name="decode",
    )(*args)


def solution(mesh):
    placed = (
        P("dp", None, "tensor", None),
        P("dp", None, "tensor", None),
        P("tensor", None, None),
        P("tensor", None, None),
        P("dp", "tensor", None),
        P("dp", None, "tensor"),
        P(None, ("dp", "tensor")),
        P("dp", "tensor"),
        P("dp"),
    )
    return jax.shard_map(
        local, mesh=mesh, in_specs=placed, out_specs=P("dp", None, "tensor", None), check_vma=False
    )
```

time: 147 us -> 37.8 us (0.26)
  matrix products: 38 us -> 0 us
  Pallas kernels: 0 us -> 36.3 us
  local copies, waits for them, and re-layouts: 37 us -> 1.32 us
  waiting for transfers between devices: 29.8 us -> 0 us
  starting transfers between devices: 20.2 us -> 0 us
  blocking collectives: 11.4 us -> 0 us
  other arithmetic: 8.91 us -> 0 us
    dot_general x5 -> x0, matrix products: 38 us -> none  [the longest x1 13.9 us: local(): jnp.einsum('rmc,rpc->rmp', latent_rows, latent_full, preferred_element_ty...]
    pallas_call x0 -> x1, Pallas kernels: none -> 36.3 us  [local(): pl.pallas_call(kernel, out_shape=jax.ShapeDtypeStruct((R, T, H, 128), BF1...]
    all_to_all x4 -> x0, waiting for transfers between devices: 29.8 us -> none  [the longest x1 27.4 us: local(): lax.all_to_all(mixture[None], 'tensor', split_axis=3, concat_axis=0, tile...]
    mul x3 -> x0, local copies, waits for them, and re-layouts: 26 us -> none  [the longest x2 26 us: local(): cache_latent.reshape(requests, blocks, block_width, groups - 1, -1)]
    all_to_all x4 -> x0, starting transfers between devices: 20.2 us -> none  [the longest x2 10.7 us: copy_for_each(): return lax.all_to_all(copies, axis, split_axis=0, concat_axis=0, tiled=True)]
    all_to_all x1 -> x0, blocking collectives: 11.4 us -> none  [copy_for_each(): return lax.all_to_all(copies, axis, split_axis=0, concat_axis=0, tiled=True)]
    reduce_sum x3 -> x0, other arithmetic: 5.82 us -> none  [the longest x1 4.65 us: local(): totals = jnp.sum(weights, axis=2).reshape(requests, new_tokens, head_count)]
    another operation x2 -> x0, local copies, waits for them, and re-layouts: 3.78 us -> none  [the longest x1 2.97 us: local(): mixture[None]]
  transfers between devices with their start and end apart: 4 -> 0, of which waited for: 2 -> 0; matrix products, arithmetic and copies ran while one was open for 33% -> 0% of each run, Pallas kernels for 0% -> 0%
where the time goes in v1:
time: 37.8 us; the launch traced here: 37.6 us
  Pallas kernels  36.3 us (96%)
  local copies, waits for them, and re-layouts  1.32 us (3%)
    pallas_call x1, Pallas kernels, local(): pl.pallas_call(kernel, out_shape=jax.ShapeDtypeStruct((R, T, H, 128), BF1...  36.3 us
    unnamed x1, local copies, waits for them, and re-layouts  1.32 us

profile of v1, /device:TPU:1, one launch (start us, length us, event | category | flops | bytes accessed | tf_op | source)
XLA Modules:
  0.0 37.6 jit_solution(15909640170830872783)
XLA Ops:
  0.0 36.3 %decode.1 = bf16[4,2,8,128]{3,2,1,0:T(8,128)(2,1)} custom-call(bf16[4,2,8,128]{3,2,1,0:T(8,128)(2,1)} %q_nope.1, bf16[4,2,8,64]{3,2,1,0:T(8,128)(2,1)} %q_rope.1, bf16[8,128,512]{2,1,0:T(8,128)(2,1)} %w_uk.1, bf16[8,512,128]{2,1,0:T(8,128)(2,1)} %w_uv.1, bf16[4,2048,512]{2,1,0:T(8,128)(2,1)} %latent.1, bf16[4,64,2048]{2,1,0:T(8,128)(2,1)} %rope.1, ...), custom_call_target="tpu_custom_call" | custom-call | tf_op jit(solution)/shard_map/decode/pallas_call | solution.py:267
  36.3 1.3 %copy.11 = bf16[4,2,8,128]{3,2,1,0:T(8,128)(2,1)} copy(bf16[4,2,8,128]{3,2,1,0:T(8,128)(2,1)} %decode.1) | data formatting | bytes 32768

commit v2 on v1

v2 whole, which is shorter than its diff:
```python
import functools
import math

import jax
import jax.numpy as jnp
from jax import lax
from jax.experimental import pallas as pl
from jax.experimental.pallas import tpu as pltpu
from jax.sharding import PartitionSpec as P

MESH = pl.DeviceIdType.MESH
R, T, H = 4, 2, 8
ROWS, LAT, ROPE, WIDE = 256, 512, 64, 640
SPAN, BLOCKS = 2048, 16
X, CHIPS = 4, 8
FACTOR = (128 + 64) ** -0.5 * math.log2(math.e)
MASKED = -1e30
UNROLL = 4
SCALE_UNROLL = 4
F32, BF16 = jnp.float32, jnp.bfloat16


ORDER = (6, 2, 5, 7, 1, 3, 4)
WIDTH = 512
CHUNKS = SPAN // WIDTH


def parts_of(value, count):
    parts = []
    for _ in range(count):
        part = value.astype(BF16).astype(F32)
        parts.append(part)
        value = value - part
    return parts


def stats_tile(peak, total):
    lane = lax.broadcasted_iota(jnp.int32, peak.shape, 1)
    tile = jnp.zeros(peak.shape, F32)
    for at, part in enumerate(parts_of(peak, 3) + parts_of(total, 2)):
        tile = jnp.where(lane == at, part, tile)
    return tile.astype(BF16)


def stats_of(tile):
    tile = tile.astype(F32)
    return tile[:, 0:1] + tile[:, 1:2] + tile[:, 2:3], tile[:, 3:4] + tile[:, 4:5]


def wide(tile):
    return jnp.concatenate([tile] * 4, axis=1)


def kernel(
    q_nope, q_rope, w_uk, w_uv, latent, rope, pool, index, lengths, out,
    nope_v, qrope_v, uk_v, uv_v, lat, rop, pool_v, table, index_s, length_s,
    qf, flat, queries, scores, weights, mixed, out_s, in_s, gains,
    out_a, in_a, out_b, in_b, out_t, in_t, att, res,
    load_sem, lat_sem, table_send, table_recv, q_send, q_recv, f_send, f_recv,
    s_send, s_recv, a_send, a_recv, t_send, t_recv, b_send, b_recv,
):
    me = lax.axis_index("tensor")
    core = lax.rem(me, 2)
    chip = me // 2
    row, column = chip // X, lax.rem(chip, X)
    partner = me + 1 - 2 * core

    def peer(j, sign):
        dy, dx = j // X, j % X
        other = lax.rem(row + dy, 2) * X + lax.rem(column + (dx if sign > 0 else X - dx), X)
        return other * 2 + core

    def remote(src, dst, send, recv, to):
        return pltpu.make_async_remote_copy(
            src_ref=src, dst_ref=dst, send_sem=send, recv_sem=recv,
            device_id={"tensor": to}, device_id_type=MESH,
        )

    barrier = pltpu.get_barrier_semaphore()
    for step in range(1, 16):
        pl.semaphore_signal(
            barrier, inc=1, device_id={"tensor": lax.rem(me + step, 16)}, device_id_type=MESH
        )

    small = [
        pltpu.make_async_copy(w_uk, uk_v, load_sem.at[0]),
        pltpu.make_async_copy(q_nope, nope_v, load_sem.at[1]),
        pltpu.make_async_copy(q_rope, qrope_v, load_sem.at[2]),
        pltpu.make_async_copy(pool, pool_v, load_sem.at[3]),
        pltpu.make_async_copy(index, index_s, load_sem.at[4]),
        pltpu.make_async_copy(lengths, length_s, load_sem.at[5]),
    ]
    big = []
    for r in range(R):
        big.append(pltpu.make_async_copy(latent.at[r], lat.at[r], lat_sem.at[r, 0]))
        big.append(pltpu.make_async_copy(rope.at[r], rop.at[r], lat_sem.at[r, 1]))
    late = pltpu.make_async_copy(w_uv, uv_v, load_sem.at[6])
    for copy in small:
        copy.start()
    with jax.named_scope("waitsmall"):
        for copy in small:
            copy.wait()
    own_table = pltpu.make_async_copy(pool_v, table.at[0], load_sem.at[7])
    for copy in [own_table] + big + [late]:
        copy.start()
    qf[...] = nope_v[...].astype(F32).reshape(R * T * H, 128)
    for h in range(H):
        rows = qf[pl.ds(h, R * T, stride=H), :].astype(BF16)
        got = jnp.dot(rows, uk_v[h], preferred_element_type=F32)
        for g in range(4):
            flat[g, pl.ds(h, R * T, stride=H), :] = got[:, 128 * g : 128 * (g + 1)]
    for r in range(R):
        for g in range(4):
            queries[r, 0:16, 128 * g : 128 * (g + 1)] = flat[g, 16 * r : 16 * (r + 1), :].astype(BF16)
        turned = qrope_v[r].astype(F32).reshape(16, ROPE)
        queries[r, 0:16, LAT:WIDE] = jnp.concatenate([turned, jnp.zeros((16, 64), F32)], axis=1).astype(BF16)

    with jax.named_scope("barrier"):
        pl.semaphore_wait(barrier, 15)
    table_copies = [
        remote(pool_v, table.at[step], table_send, table_recv, lax.rem(me + 16 - step, 16))
        for step in (8, 7, 9, 4, 5, 12, 11, 13, 3, 6, 10, 2, 14, 1, 15)
    ]
    for copy in table_copies:
        copy.start()

    q_copies = [
        [
            remote(queries.at[r, pl.ds(0, 16)], queries.at[r, pl.ds(16 * j, 16)],
                   q_send, q_recv.at[r], peer(j, -1))
            for j in ORDER
        ]
        for r in range(R)
    ]
    for r in range(R):
        for copy in q_copies[r]:
            copy.start()
    f_copies = [
        remote(queries.at[r, pl.ds(0, 128)], queries.at[r, pl.ds(128, 128)],
               f_send.at[r], f_recv.at[r], partner)
        for r in range(R)
    ]
    s_copies = [
        remote(out_s.at[r], in_s.at[r], s_send.at[r], s_recv.at[r], partner) for r in range(R)
    ]
    a_copies = [
        remote(out_a.at[r], in_a.at[r], a_send.at[r], a_recv.at[r], partner) for r in range(R)
    ]
    t_copies = [
        [
            remote(out_t.at[r, pl.ds(16 * j, 16)], in_t.at[r, pl.ds(16 * j, 16)],
                   t_send.at[r], t_recv.at[r], peer(j, 1))
            for j in ORDER
        ]
        for r in range(R)
    ]
    b_copies = [
        [
            remote(out_b.at[r, pl.ds(16 * j, 16)], in_b.at[r, pl.ds(16 * j, 16)],
                   b_send.at[r], b_recv.at[r], peer(j, 1))
            for j in ORDER
        ]
        for r in range(R)
    ]

    def seven(ref, send, recv):
        return remote(ref.at[pl.ds(16, 112)], ref.at[pl.ds(16, 112)], send, recv, partner)

    def forward(r):
        seven(queries.at[r], q_send, q_recv.at[r]).wait_recv()
        f_copies[r].start()

    with jax.named_scope("waittable"):
        remote(table.at[pl.ds(1, 15)], table.at[pl.ds(1, 15)], table_send, table_recv, partner).wait_recv()
        own_table.wait()

    def scale_block(r, b):
        at = index_s[r, b]
        slot = lax.rem(at // 64 + 16 - me, 16)
        col = lax.rem(at, 64)
        rows = pl.ds(pl.multiple_of(b * 128, 128), 128)
        for g in range(4):
            lat[r, rows, 128 * g : 128 * (g + 1)] = (
                lat[r, rows, 128 * g : 128 * (g + 1)].astype(F32) * table[slot, g, col]
            ).astype(BF16)
        rop[r, :, rows] = (rop[r, :, rows].astype(F32) * table[slot, 4, col]).astype(BF16)

    def loaded(r):
        big[2 * r].wait()
        big[2 * r + 1].wait()

    def scale(r):
        loaded(r)

        def one(b, carry):
            scale_block(r, b)
            return carry

        lax.fori_loop(0, BLOCKS, one, 0, unroll=SCALE_UNROLL)

    def score(r, n, top):
        cols = pl.ds(pl.multiple_of(n * WIDTH, WIDTH), WIDTH)
        got = lax.dot_general(
            queries[r, :, 0:LAT], lat[r, cols, :], (((1,), (1,)), ((), ())),
            preferred_element_type=F32,
        ) + jnp.dot(queries[r, :, LAT : LAT + ROPE], rop[r, :, cols], preferred_element_type=F32)
        place = lax.broadcasted_iota(jnp.int32, (1, T, 8, WIDTH), 3) + (me * SPAN + n * WIDTH)
        limit = length_s[r] - T + lax.broadcasted_iota(jnp.int32, (1, T, 8, WIDTH), 1)
        got = jnp.where(place <= limit, got.reshape(16, T, 8, WIDTH), MASKED).reshape(ROWS, WIDTH)
        scores[r % 2, :, cols] = got
        for g in range(WIDTH // 128):
            top = jnp.maximum(top, got[:, 128 * g : 128 * (g + 1)])
        return top

    def weigh(r, n, peak, total):
        cols = pl.ds(pl.multiple_of(n * WIDTH, WIDTH), WIDTH)
        got = jnp.exp2((scores[r % 2, :, cols] - peak) * FACTOR)
        weights[:, cols] = got.astype(BF16)
        for g in range(WIDTH // 128):
            total = total + got[:, 128 * g : 128 * (g + 1)]
        return total

    def both(r, peak, beside=None):
        top, total = jnp.full((ROWS, 128), -3e38, F32), jnp.zeros((ROWS, 128), F32)

        def one(n, carry):
            top, total = carry
            if r < R:
                top = score(r, n, top)
            if r > 0:
                total = weigh(r - 1, n, peak, total)
            if beside is not None:
                for b in range(BLOCKS // CHUNKS):
                    scale_block(beside, n * (BLOCKS // CHUNKS) + b)
            return top, total

        top, total = lax.fori_loop(0, CHUNKS, one, (top, total), unroll=UNROLL)
        if r < R:
            top = jnp.max(top, axis=1, keepdims=True)
        if r > 0:
            total = jnp.sum(total, axis=1, keepdims=True)
        return top, total

    def mix(r, peak, total):
        peak_w = jnp.broadcast_to(peak, (ROWS, 128))
        total_w = jnp.broadcast_to(total, (ROWS, 128))
        out_s[r, :, 0:128] = peak_w[128:]
        out_s[r, :, 128:256] = total_w[128:]
        s_copies[r].start()
        gains[r, :, 0:128] = peak_w[:128]
        gains[r, :, 128:256] = total_w[:128]
        got = jnp.dot(weights[...], lat[r], preferred_element_type=F32)
        out_a[r] = got[128:].astype(BF16)
        a_copies[r].start()
        mixed[r] = got[:128]

    def combine(r):
        with jax.named_scope(f"waits{r}"):
            s_copies[r].wait_recv()
        peak_0, total_0 = gains[r, :, 0:128], gains[r, :, 128:256]
        peak_1, total_1 = in_s[r, :, 0:128], in_s[r, :, 128:256]
        peak = jnp.maximum(peak_0, peak_1)
        gain_0 = jnp.exp2((peak_0 - peak) * FACTOR)
        gain_1 = jnp.exp2((peak_1 - peak) * FACTOR)
        out_t[r] = stats_tile(peak, total_0 * gain_0 + total_1 * gain_1)
        for copy in t_copies[r]:
            copy.start()
        with jax.named_scope(f"waita{r}"):
            a_copies[r].wait_recv()
        out_b[r] = (mixed[r] * wide(gain_0) + in_a[r].astype(F32) * wide(gain_1)).astype(BF16)
        for copy in b_copies[r]:
            copy.start()

    def finish(r):
        with jax.named_scope(f"waitt{r}"):
            seven(in_t.at[r], t_send.at[r], t_recv.at[r]).wait_recv()
        found = [stats_of(out_t[r, 0:16])] + [
            stats_of(in_t[r, 16 * j : 16 * (j + 1)]) for j in range(1, CHIPS)
        ]
        peak = functools.reduce(jnp.maximum, [p for p, _ in found])
        factors = [jnp.exp2((p - peak) * FACTOR) for p, _ in found]
        total = functools.reduce(jnp.add, [t * f for (_, t), f in zip(found, factors)])
        factors = [jnp.broadcast_to(f / total, (16, LAT)) for f in factors]
        with jax.named_scope(f"waitb{r}"):
            seven(in_b.at[r], b_send.at[r], b_recv.at[r]).wait_recv()
        attended = out_b[r, 0:16].astype(F32) * factors[0]
        for j in range(1, CHIPS):
            attended = attended + in_b[r, 16 * j : 16 * (j + 1)].astype(F32) * factors[j]
        for g in range(4):
            att[g, 16 * r : 16 * (r + 1), :] = attended[:, 128 * g : 128 * (g + 1)]

    with jax.named_scope("scale0"):
        scale(0)
    with jax.named_scope("scale1"):
        scale(1)
    with jax.named_scope("forward0"):
        forward(0)
    with jax.named_scope("scale2"):
        scale(2)
    with jax.named_scope("scale3"):
        scale(3)
    with jax.named_scope("forward1"):
        forward(1)
    with jax.named_scope("waitf0"):
        f_copies[0].wait_recv()
    with jax.named_scope("score0"):
        peak, _ = both(0, None)
    for r in range(R):
        if r + 2 < R:
            with jax.named_scope(f"forward{r+2}"):
                forward(r + 2)
        if r + 1 < R:
            with jax.named_scope(f"waitf{r+1}"):
                f_copies[r + 1].wait_recv()
        with jax.named_scope(f"both{r}"):
            next_peak, total = both(r + 1, peak)
        if r >= 1:
            combine(r - 1)
        with jax.named_scope(f"mix{r}"):
            mix(r, peak, total)
        peak = next_peak
    combine(R - 1)
    for r in range(R):
        finish(r)

    late.wait()
    for h in range(H):
        rows = jnp.concatenate(
            [att[g, pl.ds(h, R * T, stride=H), :] for g in range(4)], axis=1
        ).astype(BF16)
        res[pl.ds(h, R * T, stride=H), :] = jnp.dot(rows, uv_v[h], preferred_element_type=F32)
    out[...] = res[...].reshape(R, T, H, 128).astype(BF16)

    with jax.named_scope("drain"):
        remote(table.at[pl.ds(1, 15)], table.at[pl.ds(1, 15)], table_send, table_recv, partner).wait_send()
        for r in range(R):
            seven(queries.at[r], q_send, q_recv.at[r]).wait_send()
            f_copies[r].wait_send()
            s_copies[r].wait_send()
            a_copies[r].wait_send()
            seven(out_t.at[r], t_send.at[r], t_recv.at[r]).wait_send()
            seven(out_b.at[r], b_send.at[r], b_recv.at[r]).wait_send()


def local(*args):
    dma = pltpu.SemaphoreType.DMA
    return pl.pallas_call(
        kernel,
        out_shape=pltpu.VMEM((R, T, H, 128), BF16),
        in_specs=[pl.BlockSpec(memory_space=pl.ANY)] * 9,
        out_specs=pl.BlockSpec(memory_space=pltpu.VMEM),
        scratch_shapes=[
            pltpu.VMEM((R, T, H, 128), BF16),
            pltpu.VMEM((R, T, H, ROPE), BF16),
            pltpu.VMEM((H, 128, LAT), BF16),
            pltpu.VMEM((H, LAT, 128), BF16),
            pltpu.VMEM((R, SPAN, LAT), BF16),
            pltpu.VMEM((R, ROPE, SPAN), BF16),
            pltpu.VMEM((5, 64), F32),
            pltpu.SMEM((16, 5, 64), F32),
            pltpu.SMEM((R, BLOCKS), jnp.int32),
            pltpu.SMEM((R,), jnp.int32),
            pltpu.VMEM((R * T * H, 128), F32),
            pltpu.VMEM((4, R * T * H, 128), F32),
            pltpu.VMEM((R, ROWS, WIDE), BF16),
            pltpu.VMEM((2, ROWS, SPAN), F32),
            pltpu.VMEM((ROWS, SPAN), BF16),
            pltpu.VMEM((R, 128, LAT), F32),
            pltpu.VMEM((R, 128, 256), F32),
            pltpu.VMEM((R, 128, 256), F32),
            pltpu.VMEM((R, 128, 256), F32),
            pltpu.VMEM((R, 128, LAT), BF16),
            pltpu.VMEM((R, 128, LAT), BF16),
            pltpu.VMEM((R, 128, LAT), BF16),
            pltpu.VMEM((R, 128, LAT), BF16),
            pltpu.VMEM((R, 128, 128), BF16),
            pltpu.VMEM((R, 128, 128), BF16),
            pltpu.VMEM((4, R * T * H, 128), F32),
            pltpu.VMEM((R * T * H, 128), F32),
            dma((8,)),
            dma((R, 2)),
            dma(()),
            dma(()),
            dma(()),
            dma((R,)),
            dma((R,)),
            dma((R,)),
            dma((R,)),
            dma((R,)),
            dma((R,)),
            dma((R,)),
            dma((R,)),
            dma((R,)),
            dma((R,)),
            dma((R,)),
        ],
        compiler_params=pltpu.CompilerParams(collective_id=0, has_side_effects=True),
        name="decode",
    )(*args)


def solution(mesh):
    placed = (
        P("dp", None, "tensor", None),
        P("dp", None, "tensor", None),
        P("tensor", None, None),
        P("tensor", None, None),
        P("dp", "tensor", None),
        P("dp", None, "tensor"),
        P(None, ("dp", "tensor")),
        P("dp", "tensor"),
        P("dp"),
    )
    return jax.shard_map(
        local, mesh=mesh, in_specs=placed, out_specs=P("dp", None, "tensor", None), check_vma=False
    )
```

time: 37.8 us -> 28.2 us (0.75)
  Pallas kernels: 36.3 us -> 27.5 us
  local copies, waits for them, and re-layouts: 1.32 us -> 0.61 us
    pallas_call x1, Pallas kernels: 36.3 us -> 27.5 us  [local(): pl.pallas_call(kernel, out_shape=pltpu.VMEM((R, T, H, 128), BF16), in_spe...]
    unnamed x1, local copies, waits for them, and re-layouts: 1.32 us -> 0.61 us
where the time goes in v2:
time: 28.2 us; the launch traced here: 28.1 us
  Pallas kernels  27.5 us (98%)
  local copies, waits for them, and re-layouts  0.61 us (2%)
    pallas_call x1, Pallas kernels, local(): pl.pallas_call(kernel, out_shape=pltpu.VMEM((R, T, H, 128), BF16), in_spe...  27.5 us
    unnamed x1, local copies, waits for them, and re-layouts  0.61 us

profile of v2, /device:TPU:1, one launch (start us, length us, event | category | flops | bytes accessed | tf_op | source)
XLA Modules:
  0.0 28.1 jit_solution(9202171093980559697)
XLA Ops:
  0.0 27.5 %decode.1 = bf16[4,2,8,128]{3,2,1,0:T(8,128)(2,1)S(1)} custom-call(bf16[4,2,8,128]{3,2,1,0:T(8,128)(2,1)} %q_nope.1, bf16[4,2,8,64]{3,2,1,0:T(8,128)(2,1)} %q_rope.1, bf16[8,128,512]{2,1,0:T(8,128)(2,1)} %w_uk.1, bf16[8,512,128]{2,1,0:T(8,128)(2,1)} %w_uv.1, bf16[4,2048,512]{2,1,0:T(8,128)(2,1)} %latent.1, bf16[4,64,2048]{2,1,0:T(8,128)(2,1)} %rope.1, ...), custom_call_target="tpu_custom_call" | custom-call | tf_op jit(solution)/shard_map/decode/pallas_call | solution.py:347
  27.5 0.6 %copy.11 = bf16[4,2,8,128]{3,2,1,0:T(8,128)(2,1)} copy(bf16[4,2,8,128]{3,2,1,0:T(8,128)(2,1)S(1)} %decode.1) | data formatting | bytes 32768

commit v3 on v2

--- a/solution.py
+++ b/solution.py
@@ -10,7 +10,7 @@
 
 MESH = pl.DeviceIdType.MESH
 R, T, H = 4, 2, 8
-ROWS, LAT, ROPE, WIDE = 256, 512, 64, 640
+ROWS, LAT, ROPE = 256, 512, 64
 SPAN, BLOCKS = 2048, 16
 X, CHIPS = 4, 8
 FACTOR = (128 + 64) ** -0.5 * math.log2(math.e)
@@ -20,31 +20,18 @@
 F32, BF16 = jnp.float32, jnp.bfloat16
 
 
-ORDER = (6, 2, 5, 7, 1, 3, 4)
+ORDER = (6, 2, 5, 7, 1, 3, 4, 0)
 WIDTH = 512
 CHUNKS = SPAN // WIDTH
 
 
-def parts_of(value, count):
-    parts = []
-    for _ in range(count):
-        part = value.astype(BF16).astype(F32)
-        parts.append(part)
-        value = value - part
-    return parts
-
-
-def stats_tile(peak, total):
-    lane = lax.broadcasted_iota(jnp.int32, peak.shape, 1)
-    tile = jnp.zeros(peak.shape, F32)
-    for at, part in enumerate(parts_of(peak, 3) + parts_of(total, 2)):
-        tile = jnp.where(lane == at, part, tile)
-    return tile.astype(BF16)
-
-
-def stats_of(tile):
-    tile = tile.astype(F32)
-    return tile[:, 0:1] + tile[:, 1:2] + tile[:, 2:3], tile[:, 3:4] + tile[:, 4:5]
+def stats_rows(peak, total):
+    lane = lax.broadcasted_iota(jnp.int32, (CHIPS, 16, 128), 2)
+    at = lax.broadcasted_iota(jnp.int32, (CHIPS, 16, 128), 1)
+    spread = jnp.where(
+        lane == at, peak.reshape(CHIPS, 16, 128), jnp.where(lane == at + 16, total.reshape(CHIPS, 16, 128), 0.0)
+    )
+    return jnp.sum(spread, axis=1)
 
 
 def wide(tile):
@@ -54,9 +41,9 @@
 def kernel(
     q_nope, q_rope, w_uk, w_uv, latent, rope, pool, index, lengths, out,
     nope_v, qrope_v, uk_v, uv_v, lat, rop, pool_v, table, index_s, length_s,
-    qf, flat, queries, scores, weights, mixed, out_s, in_s, gains,
+    qf, flat, queries, turns, scores, weights, mixed, out_s, in_s, gains,
     out_a, in_a, out_b, in_b, out_t, in_t, att, res,
-    load_sem, lat_sem, table_send, table_recv, q_send, q_recv, f_send, f_recv,
+    load_sem, lat_sem, table_send, table_recv, q_send, q_recv, o_send, o_recv, f_send, f_recv, g_send, g_recv,
     s_send, s_recv, a_send, a_recv, t_send, t_recv, b_send, b_recv,
 ):
     me = lax.axis_index("tensor")
@@ -68,13 +55,16 @@
     def peer(j, sign):
         dy, dx = j // X, j % X
         other = lax.rem(row + dy, 2) * X + lax.rem(column + (dx if sign > 0 else X - dx), X)
-        return other * 2 + core
+        return other * 2 + 1 - core
 
     def remote(src, dst, send, recv, to):
         return pltpu.make_async_remote_copy(
             src_ref=src, dst_ref=dst, send_sem=send, recv_sem=recv,
             device_id={"tensor": to}, device_id_type=MESH,
         )
+
+    def eight(ref, send, recv):
+        return remote(ref.at[pl.ds(0, 128)], ref.at[pl.ds(0, 128)], send, recv, partner)
 
     barrier = pltpu.get_barrier_semaphore()
     for step in range(1, 16):
@@ -90,10 +80,8 @@
         pltpu.make_async_copy(index, index_s, load_sem.at[4]),
         pltpu.make_async_copy(lengths, length_s, load_sem.at[5]),
     ]
-    big = []
-    for r in range(R):
-        big.append(pltpu.make_async_copy(latent.at[r], lat.at[r], lat_sem.at[r, 0]))
-        big.append(pltpu.make_async_copy(rope.at[r], rop.at[r], lat_sem.at[r, 1]))
+    big = [pltpu.make_async_copy(latent.at[r], lat.at[r], lat_sem.at[r]) for r in range(R)]
+    big.insert(1, pltpu.make_async_copy(rope, rop, lat_sem.at[R]))
     late = pltpu.make_async_copy(w_uv, uv_v, load_sem.at[6])
     for copy in small:
         copy.start()
@@ -111,9 +99,11 @@
             flat[g, pl.ds(h, R * T, stride=H), :] = got[:, 128 * g : 128 * (g + 1)]
     for r in range(R):
         for g in range(4):
-            queries[r, 0:16, 128 * g : 128 * (g + 1)] = flat[g, 16 * r : 16 * (r + 1), :].astype(BF16)
-        turned = qrope_v[r].astype(F32).reshape(16, ROPE)
-        queries[r, 0:16, LAT:WIDE] = jnp.concatenate([turned, jnp.zeros((16, 64), F32)], axis=1).astype(BF16)
+            queries[r, 128:144, 128 * g : 128 * (g + 1)] = flat[g, 16 * r : 16 * (r + 1), :].astype(BF16)
+
+    for pair in range(R // 2):
+        turned = [qrope_v[2 * pair + n].astype(F32).reshape(16, ROPE) for n in range(2)]
+        turns[pair, 128:144] = jnp.concatenate(turned, axis=1).astype(BF16)
 
     with jax.named_scope("barrier"):
         pl.semaphore_wait(barrier, 15)
@@ -126,30 +116,43 @@
 
     q_copies = [
         [
-            remote(queries.at[r, pl.ds(0, 16)], queries.at[r, pl.ds(16 * j, 16)],
+            remote(queries.at[r, pl.ds(128, 16)], queries.at[r, pl.ds(16 * j, 16)],
                    q_send, q_recv.at[r], peer(j, -1))
             for j in ORDER
         ]
         for r in range(R)
     ]
+    o_copies = [
+        [
+            remote(turns.at[p, pl.ds(128, 16)], turns.at[p, pl.ds(16 * j, 16)], o_send, o_recv.at[p], peer(j, -1))
+            for j in ORDER
+        ]
+        for p in range(R // 2)
+    ]
     for r in range(R):
-        for copy in q_copies[r]:
-            copy.start()
+        for at in range(CHIPS):
+            if r % 2 == 0:
+                o_copies[r // 2][at].start()
+            q_copies[r][at].start()
+    g_copies = [
+        remote(turns.at[p, pl.ds(16, 112)], turns.at[p, pl.ds(144, 112)], g_send, g_recv.at[p], partner)
+        for p in range(R // 2)
+    ]
     f_copies = [
-        remote(queries.at[r, pl.ds(0, 128)], queries.at[r, pl.ds(128, 128)],
-               f_send.at[r], f_recv.at[r], partner)
+        remote(queries.at[r, pl.ds(16, 112)], queries.at[r, pl.ds(144, 112)],
+               f_send, f_recv.at[r], partner)
         for r in range(R)
     ]
     s_copies = [
-        remote(out_s.at[r], in_s.at[r], s_send.at[r], s_recv.at[r], partner) for r in range(R)
+        remote(out_s.at[r], in_s.at[r], s_send, s_recv.at[r], partner) for r in range(R)
     ]
     a_copies = [
-        remote(out_a.at[r], in_a.at[r], a_send.at[r], a_recv.at[r], partner) for r in range(R)
+        remote(out_a.at[r], in_a.at[r], a_send, a_recv.at[r], partner) for r in range(R)
     ]
     t_copies = [
         [
-            remote(out_t.at[r, pl.ds(16 * j, 16)], in_t.at[r, pl.ds(16 * j, 16)],
-                   t_send.at[r], t_recv.at[r], peer(j, 1))
+            remote(out_t.at[r, pl.ds(j, 1)], in_t.at[r, pl.ds(j, 1)],
+                   t_send, t_recv.at[r], peer(j, 1))
             for j in ORDER
         ]
         for r in range(R)
@@ -157,18 +160,23 @@
     b_copies = [
         [
             remote(out_b.at[r, pl.ds(16 * j, 16)], in_b.at[r, pl.ds(16 * j, 16)],
-                   b_send.at[r], b_recv.at[r], peer(j, 1))
+                   b_send, b_recv.at[r], peer(j, 1))
             for j in ORDER
         ]
         for r in range(R)
     ]
 
-    def seven(ref, send, recv):
-        return remote(ref.at[pl.ds(16, 112)], ref.at[pl.ds(16, 112)], send, recv, partner)
-
     def forward(r):
-        seven(queries.at[r], q_send, q_recv.at[r]).wait_recv()
+        if r % 2 == 0:
+            eight(turns.at[r // 2], o_send, o_recv.at[r // 2]).wait_recv()
+            g_copies[r // 2].start()
+        eight(queries.at[r], q_send, q_recv.at[r]).wait_recv()
         f_copies[r].start()
+
+    def forwarded(r):
+        if r % 2 == 0:
+            g_copies[r // 2].wait_recv()
+        f_copies[r].wait_recv()
 
     with jax.named_scope("waittable"):
         remote(table.at[pl.ds(1, 15)], table.at[pl.ds(1, 15)], table_send, table_recv, partner).wait_recv()
@@ -185,25 +193,26 @@
             ).astype(BF16)
         rop[r, :, rows] = (rop[r, :, rows].astype(F32) * table[slot, 4, col]).astype(BF16)
 
-    def loaded(r):
-        big[2 * r].wait()
-        big[2 * r + 1].wait()
-
-    def scale(r):
-        loaded(r)
+    def scale(r, first=0, last=BLOCKS):
+        if first == 0:
+            big[r + 1 if r else 0].wait()
+            if r == 0:
+                big[1].wait()
 
         def one(b, carry):
             scale_block(r, b)
             return carry
 
-        lax.fori_loop(0, BLOCKS, one, 0, unroll=SCALE_UNROLL)
+        lax.fori_loop(first, last, one, 0, unroll=SCALE_UNROLL)
 
     def score(r, n, top):
         cols = pl.ds(pl.multiple_of(n * WIDTH, WIDTH), WIDTH)
         got = lax.dot_general(
-            queries[r, :, 0:LAT], lat[r, cols, :], (((1,), (1,)), ((), ())),
+            queries[r], lat[r, cols, :], (((1,), (1,)), ((), ())),
             preferred_element_type=F32,
-        ) + jnp.dot(queries[r, :, LAT : LAT + ROPE], rop[r, :, cols], preferred_element_type=F32)
+        ) + jnp.dot(
+            turns[r // 2, :, ROPE * (r % 2) : ROPE * (r % 2 + 1)], rop[r, :, cols], preferred_element_type=F32
+        )
         place = lax.broadcasted_iota(jnp.int32, (1, T, 8, WIDTH), 3) + (me * SPAN + n * WIDTH)
         limit = length_s[r] - T + lax.broadcasted_iota(jnp.int32, (1, T, 8, WIDTH), 1)
         got = jnp.where(place <= limit, got.reshape(16, T, 8, WIDTH), MASKED).reshape(ROWS, WIDTH)
@@ -262,7 +271,7 @@
         peak = jnp.maximum(peak_0, peak_1)
         gain_0 = jnp.exp2((peak_0 - peak) * FACTOR)
         gain_1 = jnp.exp2((peak_1 - peak) * FACTOR)
-        out_t[r] = stats_tile(peak, total_0 * gain_0 + total_1 * gain_1)
+        out_t[r] = stats_rows(peak, total_0 * gain_0 + total_1 * gain_1)
         for copy in t_copies[r]:
             copy.start()
         with jax.named_scope(f"waita{r}"):
@@ -273,18 +282,17 @@
 
     def finish(r):
         with jax.named_scope(f"waitt{r}"):
-            seven(in_t.at[r], t_send.at[r], t_recv.at[r]).wait_recv()
-        found = [stats_of(out_t[r, 0:16])] + [
-            stats_of(in_t[r, 16 * j : 16 * (j + 1)]) for j in range(1, CHIPS)
-        ]
-        peak = functools.reduce(jnp.maximum, [p for p, _ in found])
-        factors = [jnp.exp2((p - peak) * FACTOR) for p, _ in found]
-        total = functools.reduce(jnp.add, [t * f for (_, t), f in zip(found, factors)])
-        factors = [jnp.broadcast_to(f / total, (16, LAT)) for f in factors]
+            remote(out_t.at[r], in_t.at[r], t_send, t_recv.at[r], partner).wait_recv()
+        found = in_t[r]
+        factors = jnp.exp2((found - jnp.max(found, axis=0, keepdims=True)) * FACTOR)
+        total = jnp.sum(factors * pltpu.roll(found, 112, 1), axis=0, keepdims=True)
+        lane = lax.broadcasted_iota(jnp.int32, (CHIPS, 128), 1)
+        factors = jnp.transpose(jnp.where(lane < 16, factors / total, 0.0))[0:16]
+        factors = [jnp.broadcast_to(factors[:, j : j + 1], (16, LAT)) for j in range(CHIPS)]
         with jax.named_scope(f"waitb{r}"):
-            seven(in_b.at[r], b_send.at[r], b_recv.at[r]).wait_recv()
-        attended = out_b[r, 0:16].astype(F32) * factors[0]
-        for j in range(1, CHIPS):
+            eight(in_b.at[r], b_send, b_recv.at[r]).wait_recv()
+        attended = jnp.zeros((16, LAT), F32)
+        for j in range(CHIPS):
             attended = attended + in_b[r, 16 * j : 16 * (j + 1)].astype(F32) * factors[j]
         for g in range(4):
             att[g, 16 * r : 16 * (r + 1), :] = attended[:, 128 * g : 128 * (g + 1)]
@@ -292,17 +300,18 @@
     with jax.named_scope("scale0"):
         scale(0)
     with jax.named_scope("scale1"):
-        scale(1)
+        scale(1, 0, 8)
     with jax.named_scope("forward0"):
         forward(0)
     with jax.named_scope("scale2"):
+        scale(1, 8, 16)
         scale(2)
     with jax.named_scope("scale3"):
         scale(3)
     with jax.named_scope("forward1"):
         forward(1)
     with jax.named_scope("waitf0"):
-        f_copies[0].wait_recv()
+        forwarded(0)
     with jax.named_scope("score0"):
         peak, _ = both(0, None)
     for r in range(R):
@@ -311,13 +320,15 @@
                 forward(r + 2)
         if r + 1 < R:
             with jax.named_scope(f"waitf{r+1}"):
-                f_copies[r + 1].wait_recv()
+                forwarded(r + 1)
         with jax.named_scope(f"both{r}"):
             next_peak, total = both(r + 1, peak)
-        if r >= 1:
+        if 1 <= r < R - 1:
             combine(r - 1)
         with jax.named_scope(f"mix{r}"):
             mix(r, peak, total)
+        if r == R - 1:
+            combine(r - 1)
         peak = next_peak
     combine(R - 1)
     for r in range(R):
@@ -333,13 +344,12 @@
 
     with jax.named_scope("drain"):
         remote(table.at[pl.ds(1, 15)], table.at[pl.ds(1, 15)], table_send, table_recv, partner).wait_send()
-        for r in range(R):
-            seven(queries.at[r], q_send, q_recv.at[r]).wait_send()
-            f_copies[r].wait_send()
-            s_copies[r].wait_send()
-            a_copies[r].wait_send()
-            seven(out_t.at[r], t_send.at[r], t_recv.at[r]).wait_send()
-            seven(out_b.at[r], b_send.at[r], b_recv.at[r]).wait_send()
+        for ref, rows, send in (
+            (queries, pl.ds(0, 128), q_send), (turns, pl.ds(0, 128), o_send), (turns, pl.ds(16, 112), g_send),
+            (queries, pl.ds(16, 112), f_send), (out_s, pl.ds(0, 128), s_send),
+            (out_a, pl.ds(0, 128), a_send), (out_t, pl.ds(0, 8), t_send), (out_b, pl.ds(0, 128), b_send),
+        ):
+            remote(ref.at[:, rows], ref.at[:, rows], send, table_recv, partner).wait_send()
 
 
 def local(*args):
@@ -362,7 +372,8 @@
             pltpu.SMEM((R,), jnp.int32),
             pltpu.VMEM((R * T * H, 128), F32),
             pltpu.VMEM((4, R * T * H, 128), F32),
-            pltpu.VMEM((R, ROWS, WIDE), BF16),
+            pltpu.VMEM((R, ROWS, LAT), BF16),
+            pltpu.VMEM((R // 2, ROWS, 128), BF16),
             pltpu.VMEM((2, ROWS, SPAN), F32),
             pltpu.VMEM((ROWS, SPAN), BF16),
             pltpu.VMEM((R, 128, LAT), F32),
@@ -373,25 +384,29 @@
             pltpu.VMEM((R, 128, LAT), BF16),
             pltpu.VMEM((R, 128, LAT), BF16),
             pltpu.VMEM((R, 128, LAT), BF16),
-            pltpu.VMEM((R, 128, 128), BF16),
-            pltpu.VMEM((R, 128, 128), BF16),
+            pltpu.VMEM((R, CHIPS, 128), F32),
+            pltpu.VMEM((R, CHIPS, 128), F32),
             pltpu.VMEM((4, R * T * H, 128), F32),
             pltpu.VMEM((R * T * H, 128), F32),
             dma((8,)),
-            dma((R, 2)),
-            dma(()),
-            dma(()),
-            dma(()),
-            dma((R,)),
-            dma((R,)),
-            dma((R,)),
-            dma((R,)),
-            dma((R,)),
-            dma((R,)),
-            dma((R,)),
-            dma((R,)),
-            dma((R,)),
-            dma((R,)),
+            dma((R + 1,)),
+            dma(()),
+            dma(()),
+            dma(()),
+            dma((R,)),
+            dma(()),
+            dma((R // 2,)),
+            dma(()),
+            dma((R,)),
+            dma(()),
+            dma((R // 2,)),
+            dma(()),
+            dma((R,)),
+            dma(()),
+            dma((R,)),
+            dma(()),
+            dma((R,)),
+            dma(()),
             dma((R,)),
         ],
         compiler_params=pltpu.CompilerParams(collective_id=0, has_side_effects=True),

time: 28.2 us -> 27.1 us (0.961)
  Pallas kernels: 27.5 us -> 26.4 us
    pallas_call x1, Pallas kernels: 27.5 us -> 26.4 us  [local(): pl.pallas_call(kernel, out_shape=pltpu.VMEM((R, T, H, 128), BF16), in_spe...]
where the time goes in v3:
time: 27.1 us; the launch traced here: 27 us
  Pallas kernels  26.4 us (97%)
  local copies, waits for them, and re-layouts  0.61 us (2%)
    pallas_call x1, Pallas kernels, local(): pl.pallas_call(kernel, out_shape=pltpu.VMEM((R, T, H, 128), BF16), in_spe...  26.4 us
    unnamed x1, local copies, waits for them, and re-layouts  0.61 us

profile of v3, /device:TPU:1, one launch (start us, length us, event | category | flops | bytes accessed | tf_op | source)
XLA Modules:
  0.0 27.0 jit_solution(4979648952206521283)
XLA Ops:
  0.0 26.4 %decode.1 = bf16[4,2,8,128]{3,2,1,0:T(8,128)(2,1)S(1)} custom-call(bf16[4,2,8,128]{3,2,1,0:T(8,128)(2,1)} %q_nope.1, bf16[4,2,8,64]{3,2,1,0:T(8,128)(2,1)} %q_rope.1, bf16[8,128,512]{2,1,0:T(8,128)(2,1)} %w_uk.1, bf16[8,512,128]{2,1,0:T(8,128)(2,1)} %w_uv.1, bf16[4,2048,512]{2,1,0:T(8,128)(2,1)} %latent.1, bf16[4,64,2048]{2,1,0:T(8,128)(2,1)} %rope.1, ...), custom_call_target="tpu_custom_call" | custom-call | tf_op jit(solution)/shard_map/decode/pallas_call | solution.py:357
  26.4 0.6 %copy.11 = bf16[4,2,8,128]{3,2,1,0:T(8,128)(2,1)} copy(bf16[4,2,8,128]{3,2,1,0:T(8,128)(2,1)S(1)} %decode.1) | data formatting | bytes 32768

commit v4 on v3

--- a/solution.py
+++ b/solution.py
@@ -15,7 +15,8 @@
 X, CHIPS = 4, 8
 FACTOR = (128 + 64) ** -0.5 * math.log2(math.e)
 MASKED = -1e30
-UNROLL = 4
+MERGE = True
+SPLIT = 8
 SCALE_UNROLL = 4
 F32, BF16 = jnp.float32, jnp.bfloat16
 
@@ -129,11 +130,16 @@
         ]
         for p in range(R // 2)
     ]
-    for r in range(R):
+    def ask(r):
         for at in range(CHIPS):
             if r % 2 == 0:
                 o_copies[r // 2][at].start()
             q_copies[r][at].start()
+
+    ask(0)
+    ask(1)
+    ask(2)
+    ask(3)
     g_copies = [
         remote(turns.at[p, pl.ds(16, 112)], turns.at[p, pl.ds(144, 112)], g_send, g_recv.at[p], partner)
         for p in range(R // 2)
@@ -194,7 +200,7 @@
         rop[r, :, rows] = (rop[r, :, rows].astype(F32) * table[slot, 4, col]).astype(BF16)
 
     def scale(r, first=0, last=BLOCKS):
-        if first == 0:
+        if first == 0 and last > 0:
             big[r + 1 if r else 0].wait()
             if r == 0:
                 big[1].wait()
@@ -206,7 +212,7 @@
         lax.fori_loop(first, last, one, 0, unroll=SCALE_UNROLL)
 
     def score(r, n, top):
-        cols = pl.ds(pl.multiple_of(n * WIDTH, WIDTH), WIDTH)
+        cols = pl.ds(n * WIDTH, WIDTH)
         got = lax.dot_general(
             queries[r], lat[r, cols, :], (((1,), (1,)), ((), ())),
             preferred_element_type=F32,
@@ -222,35 +228,22 @@
         return top
 
     def weigh(r, n, peak, total):
-        cols = pl.ds(pl.multiple_of(n * WIDTH, WIDTH), WIDTH)
+        cols = pl.ds(n * WIDTH, WIDTH)
         got = jnp.exp2((scores[r % 2, :, cols] - peak) * FACTOR)
         weights[:, cols] = got.astype(BF16)
         for g in range(WIDTH // 128):
             total = total + got[:, 128 * g : 128 * (g + 1)]
         return total
 
-    def both(r, peak, beside=None):
-        top, total = jnp.full((ROWS, 128), -3e38, F32), jnp.zeros((ROWS, 128), F32)
-
-        def one(n, carry):
-            top, total = carry
-            if r < R:
-                top = score(r, n, top)
-            if r > 0:
-                total = weigh(r - 1, n, peak, total)
-            if beside is not None:
-                for b in range(BLOCKS // CHUNKS):
-                    scale_block(beside, n * (BLOCKS // CHUNKS) + b)
-            return top, total
-
-        top, total = lax.fori_loop(0, CHUNKS, one, (top, total), unroll=UNROLL)
-        if r < R:
-            top = jnp.max(top, axis=1, keepdims=True)
-        if r > 0:
-            total = jnp.sum(total, axis=1, keepdims=True)
-        return top, total
-
-    def mix(r, peak, total):
+    def look(r, between=None):
+        top = jnp.full((ROWS, 128), -3e38, F32)
+        for n in range(CHUNKS):
+            if between is not None and n == between[0]:
+                between[1]()
+            top = score(r, n, top)
+        return jnp.max(top, axis=1, keepdims=True)
+
+    def tell(r, peak, total):
         peak_w = jnp.broadcast_to(peak, (ROWS, 128))
         total_w = jnp.broadcast_to(total, (ROWS, 128))
         out_s[r, :, 0:128] = peak_w[128:]
@@ -258,27 +251,58 @@
         s_copies[r].start()
         gains[r, :, 0:128] = peak_w[:128]
         gains[r, :, 128:256] = total_w[:128]
-        got = jnp.dot(weights[...], lat[r], preferred_element_type=F32)
+
+    def keep(r, got):
         out_a[r] = got[128:].astype(BF16)
         a_copies[r].start()
         mixed[r] = got[:128]
 
-    def combine(r):
-        with jax.named_scope(f"waits{r}"):
-            s_copies[r].wait_recv()
+    def factors_of(r):
         peak_0, total_0 = gains[r, :, 0:128], gains[r, :, 128:256]
         peak_1, total_1 = in_s[r, :, 0:128], in_s[r, :, 128:256]
         peak = jnp.maximum(peak_0, peak_1)
         gain_0 = jnp.exp2((peak_0 - peak) * FACTOR)
         gain_1 = jnp.exp2((peak_1 - peak) * FACTOR)
         out_t[r] = stats_rows(peak, total_0 * gain_0 + total_1 * gain_1)
+        return gain_0, gain_1
+
+    def join(r, gain_0, gain_1):
+        out_b[r] = (mixed[r] * wide(gain_0) + in_a[r].astype(F32) * wide(gain_1)).astype(BF16)
+
+    def combine(r):
+        with jax.named_scope(f"waits{r}"):
+            s_copies[r].wait_recv()
+        both_gains = factors_of(r)
         for copy in t_copies[r]:
             copy.start()
         with jax.named_scope(f"waita{r}"):
             a_copies[r].wait_recv()
-        out_b[r] = (mixed[r] * wide(gain_0) + in_a[r].astype(F32) * wide(gain_1)).astype(BF16)
+        join(r, *both_gains)
         for copy in b_copies[r]:
             copy.start()
+
+    def mix(r, peak):
+        if r >= 1 and MERGE:
+            with jax.named_scope(f"waitsa{r-1}"):
+                s_copies[r - 1].wait_recv()
+                a_copies[r - 1].wait_recv()
+        elif r >= 1:
+            combine(r - 1)
+        with jax.named_scope(f"mix{r}"):
+            total, got = jnp.zeros((ROWS, 128), F32), None
+            for n in range(CHUNKS):
+                total = weigh(r, n, peak, total)
+            if r >= 1 and MERGE:
+                join(r - 1, *factors_of(r - 1))
+            for n in range(CHUNKS):
+                cols = pl.ds(n * WIDTH, WIDTH)
+                one = jnp.dot(weights[:, cols], lat[r, cols, :], preferred_element_type=F32)
+                got = one if got is None else got + one
+            if r >= 1 and MERGE:
+                for copy in t_copies[r - 1] + b_copies[r - 1]:
+                    copy.start()
+            tell(r, peak, jnp.sum(total, axis=1, keepdims=True))
+            keep(r, got)
 
     def finish(r):
         with jax.named_scope(f"waitt{r}"):
@@ -306,30 +330,16 @@
     with jax.named_scope("scale2"):
         scale(1, 8, 16)
         scale(2)
-    with jax.named_scope("scale3"):
-        scale(3)
-    with jax.named_scope("forward1"):
-        forward(1)
-    with jax.named_scope("waitf0"):
-        forwarded(0)
-    with jax.named_scope("score0"):
-        peak, _ = both(0, None)
+    scale(3, 0, SPLIT)
     for r in range(R):
-        if r + 2 < R:
-            with jax.named_scope(f"forward{r+2}"):
-                forward(r + 2)
-        if r + 1 < R:
-            with jax.named_scope(f"waitf{r+1}"):
-                forwarded(r + 1)
-        with jax.named_scope(f"both{r}"):
-            next_peak, total = both(r + 1, peak)
-        if 1 <= r < R - 1:
-            combine(r - 1)
-        with jax.named_scope(f"mix{r}"):
-            mix(r, peak, total)
-        if r == R - 1:
-            combine(r - 1)
-        peak = next_peak
+        with jax.named_scope(f"waitf{r}"):
+            forwarded(r)
+        with jax.named_scope(f"score{r}"):
+            peak = look(r, (1, functools.partial(forward, r + 1)) if r + 1 < R else None)
+        if r == 0:
+            with jax.named_scope("scale3"):
+                scale(3, SPLIT, BLOCKS)
+        mix(r, peak)
     combine(R - 1)
     for r in range(R):
         finish(r)

time: 27.1 us -> 26.7 us (0.985)
  Pallas kernels: 26.4 us -> 26 us
    pallas_call x1, Pallas kernels: 26.4 us -> 26 us  [local(): pl.pallas_call(kernel, out_shape=pltpu.VMEM((R, T, H, 128), BF16), in_spe...]
where the time goes in v4:
time: 26.7 us; the launch traced here: 26.6 us
  Pallas kernels  26 us (97%)
  local copies, waits for them, and re-layouts  0.61 us (2%)
    pallas_call x1, Pallas kernels, local(): pl.pallas_call(kernel, out_shape=pltpu.VMEM((R, T, H, 128), BF16), in_spe...  26 us
    unnamed x1, local copies, waits for them, and re-layouts  0.61 us

profile of v4, /device:TPU:1, one launch (start us, length us, event | category | flops | bytes accessed | tf_op | source)
XLA Modules:
  0.0 26.6 jit_solution(10666005643177381124)
XLA Ops:
  0.0 26.0 %decode.1 = bf16[4,2,8,128]{3,2,1,0:T(8,128)(2,1)S(1)} custom-call(bf16[4,2,8,128]{3,2,1,0:T(8,128)(2,1)} %q_nope.1, bf16[4,2,8,64]{3,2,1,0:T(8,128)(2,1)} %q_rope.1, bf16[8,128,512]{2,1,0:T(8,128)(2,1)} %w_uk.1, bf16[8,512,128]{2,1,0:T(8,128)(2,1)} %w_uv.1, bf16[4,2048,512]{2,1,0:T(8,128)(2,1)} %latent.1, bf16[4,64,2048]{2,1,0:T(8,128)(2,1)} %rope.1, ...), custom_call_target="tpu_custom_call" | custom-call | tf_op jit(solution)/shard_map/decode/pallas_call | solution.py:367
  26.0 0.6 %copy.11 = bf16[4,2,8,128]{3,2,1,0:T(8,128)(2,1)} copy(bf16[4,2,8,128]{3,2,1,0:T(8,128)(2,1)S(1)} %decode.1) | data formatting | bytes 32768

commit v5 on v4

--- a/solution.py
+++ b/solution.py
@@ -227,10 +227,10 @@
             top = jnp.maximum(top, got[:, 128 * g : 128 * (g + 1)])
         return top
 
-    def weigh(r, n, peak, total):
+    def weigh(r, n, peak, total, rows=slice(0, ROWS)):
         cols = pl.ds(n * WIDTH, WIDTH)
-        got = jnp.exp2((scores[r % 2, :, cols] - peak) * FACTOR)
-        weights[:, cols] = got.astype(BF16)
+        got = jnp.exp2((scores[r % 2, rows, cols] - peak[rows]) * FACTOR)
+        weights[rows, cols] = got.astype(BF16)
         for g in range(WIDTH // 128):
             total = total + got[:, 128 * g : 128 * (g + 1)]
         return total
@@ -280,6 +280,32 @@
         join(r, *both_gains)
         for copy in b_copies[r]:
             copy.start()
+
+    def mix_last(r, peak):
+        with jax.named_scope(f"waitsa{r-1}"):
+            s_copies[r - 1].wait_recv()
+            a_copies[r - 1].wait_recv()
+        with jax.named_scope(f"mix{r}"):
+            join(r - 1, *factors_of(r - 1))
+            peak_w = jnp.broadcast_to(peak, (ROWS, 128))
+            for rows in (slice(128, 256), slice(0, 128)):
+                total, got = jnp.zeros((128, 128), F32), None
+                for n in range(CHUNKS):
+                    total = weigh(r, n, peak, total, rows)
+                got = jnp.dot(weights[rows], lat[r], preferred_element_type=F32)
+                total_w = jnp.broadcast_to(jnp.sum(total, axis=1, keepdims=True), (128, 128))
+                if rows.start:
+                    out_s[r, :, 0:128] = peak_w[128:]
+                    out_s[r, :, 128:256] = total_w
+                    s_copies[r].start()
+                    out_a[r] = got.astype(BF16)
+                    a_copies[r].start()
+                    for copy in t_copies[r - 1] + b_copies[r - 1]:
+                        copy.start()
+                else:
+                    gains[r, :, 0:128] = peak_w[:128]
+                    gains[r, :, 128:256] = total_w
+                    mixed[r] = got
 
     def mix(r, peak):
         if r >= 1 and MERGE:
@@ -333,13 +359,15 @@
     scale(3, 0, SPLIT)
     for r in range(R):
         with jax.named_scope(f"waitf{r}"):
+            if 1 <= r < R - 1:
+                forward(r + 1)
             forwarded(r)
         with jax.named_scope(f"score{r}"):
-            peak = look(r, (1, functools.partial(forward, r + 1)) if r + 1 < R else None)
+            peak = look(r, (1, functools.partial(forward, 1)) if r == 0 else None)
         if r == 0:
             with jax.named_scope("scale3"):
                 scale(3, SPLIT, BLOCKS)
-        mix(r, peak)
+        mix_last(r, peak) if r == R - 1 else mix(r, peak)
     combine(R - 1)
     for r in range(R):
         finish(r)

time: 26.7 us -> 26.6 us (level)
  no operation moved by 1% of the time
where the time goes in v5:
time: 26.6 us; the launch traced here: 26.5 us
  Pallas kernels  25.9 us (97%)
  local copies, waits for them, and re-layouts  0.61 us (2%)
    pallas_call x1, Pallas kernels, local(): pl.pallas_call(kernel, out_shape=pltpu.VMEM((R, T, H, 128), BF16), in_spe...  25.9 us
    unnamed x1, local copies, waits for them, and re-layouts  0.61 us

profile of v5, /device:TPU:1, one launch (start us, length us, event | category | flops | bytes accessed | tf_op | source)
XLA Modules:
  0.0 26.5 jit_solution(7061888449313116880)
XLA Ops:
  0.0 25.9 %decode.1 = bf16[4,2,8,128]{3,2,1,0:T(8,128)(2,1)S(1)} custom-call(bf16[4,2,8,128]{3,2,1,0:T(8,128)(2,1)} %q_nope.1, bf16[4,2,8,64]{3,2,1,0:T(8,128)(2,1)} %q_rope.1, bf16[8,128,512]{2,1,0:T(8,128)(2,1)} %w_uk.1, bf16[8,512,128]{2,1,0:T(8,128)(2,1)} %w_uv.1, bf16[4,2048,512]{2,1,0:T(8,128)(2,1)} %latent.1, bf16[4,64,2048]{2,1,0:T(8,128)(2,1)} %rope.1, ...), custom_call_target="tpu_custom_call" | custom-call | tf_op jit(solution)/shard_map/decode/pallas_call | solution.py:395
  25.9 0.6 %copy.11 = bf16[4,2,8,128]{3,2,1,0:T(8,128)(2,1)} copy(bf16[4,2,8,128]{3,2,1,0:T(8,128)(2,1)S(1)} %decode.1) | data formatting | bytes 32768

commit v6 on v5

--- a/solution.py
+++ b/solution.py
@@ -277,8 +277,12 @@
             copy.start()
         with jax.named_scope(f"waita{r}"):
             a_copies[r].wait_recv()
-        join(r, *both_gains)
-        for copy in b_copies[r]:
+        gain_0, gain_1 = both_gains
+        for j, copy in zip(ORDER, b_copies[r]):
+            rows = slice(16 * j, 16 * (j + 1))
+            out_b[r, rows] = (
+                mixed[r, rows] * wide(gain_0[rows]) + in_a[r, rows].astype(F32) * wide(gain_1[rows])
+            ).astype(BF16)
             copy.start()
 
     def mix_last(r, peak):

time: 26.6 us -> 26.5 us (level)
  no operation moved by 1% of the time
where the time goes in v6:
time: 26.5 us; the launch traced here: 26.4 us
  Pallas kernels  25.8 us (97%)
  local copies, waits for them, and re-layouts  0.61 us (2%)
    pallas_call x1, Pallas kernels, local(): pl.pallas_call(kernel, out_shape=pltpu.VMEM((R, T, H, 128), BF16), in_spe...  25.8 us
    unnamed x1, local copies, waits for them, and re-layouts  0.61 us

profile of v6, /device:TPU:1, one launch (start us, length us, event | category | flops | bytes accessed | tf_op | source)
XLA Modules:
  0.0 26.4 jit_solution(17119123854093310425)
XLA Ops:
  0.0 25.8 %decode.1 = bf16[4,2,8,128]{3,2,1,0:T(8,128)(2,1)S(1)} custom-call(bf16[4,2,8,128]{3,2,1,0:T(8,128)(2,1)} %q_nope.1, bf16[4,2,8,64]{3,2,1,0:T(8,128)(2,1)} %q_rope.1, bf16[8,128,512]{2,1,0:T(8,128)(2,1)} %w_uk.1, bf16[8,512,128]{2,1,0:T(8,128)(2,1)} %w_uv.1, bf16[4,2048,512]{2,1,0:T(8,128)(2,1)} %latent.1, bf16[4,64,2048]{2,1,0:T(8,128)(2,1)} %rope.1, ...), custom_call_target="tpu_custom_call" | custom-call | tf_op jit(solution)/shard_map/decode/pallas_call | solution.py:399
  25.8 0.6 %copy.11 = bf16[4,2,8,128]{3,2,1,0:T(8,128)(2,1)} copy(bf16[4,2,8,128]{3,2,1,0:T(8,128)(2,1)S(1)} %decode.1) | data formatting | bytes 32768
